TPU v7x, 512 devices: a whole 4x8x8 slice. The times are simulated.
512 devices in a mesh: dp: 8 (over z), ctx: 4 (over y_lo, core), tp: 16 (over y_hi, x).
Axes of the slice: x: 4, y: 8 (y_hi: 4, y_lo: 2; y = y_hi * 2 + y_lo), z: 8, core: 2. Of those that a mesh axis runs over, the one named last changes fastest.
Arguments:
- layer_input: bfloat16 [8, 1024, 8192], P('dp', ('ctx', 'tp')), may hold values from -6 to 6
- value_weight: bfloat16 [8192, 4096], P(('dp', 'ctx'), 'tp'), may hold values from -0.0625 to 0.0625
- query_raw: bfloat16 [8, 1024, 4096], P('dp', 'ctx', 'tp'), may hold values from -6 to 6
- key_raw: bfloat16 [8, 1024, 4096], P('dp', 'ctx', 'tp'), may hold values from -6 to 6
- out_grad: bfloat16 [8, 1024, 4096], P('dp', 'ctx', 'tp'), may hold values from -6 to 6
- gate_logits: float32 [2, 8, 32, 1024], P(None, 'dp', 'tp', 'ctx'), may hold values from -14 to 4, as said below
- decay_params: float32 [2, 32], P(None, 'tp'), may hold values from -0.35 to 0.35
- saved_states: float32 [8, 4, 32, 128, 128], P('dp', 'ctx', 'tp'), may hold values from -4 to 4
Outputs:
- input_grad: bfloat16 [8, 1024, 8192], P('dp', ('ctx', 'tp'))
- query_grad: bfloat16 [8, 1024, 4096], P('dp', 'ctx', 'tp')
- key_grad: bfloat16 [8, 1024, 4096], P('dp', 'ctx', 'tp')
- gate_grad: float32 [2, 8, 32, 1024], P(None, 'dp', 'tp', 'ctx')
- decay_grad: float32 [2, 32], P(None, 'tp')
Inputs may be any that keep to these rules, and one draw needn't show every extreme that they name: `gate_logits`: row 0 holds decay logits, row 1 write-strength logits.
All inputs are finite; a program needn't handle non-finite values.
Results may differ from a plain program's by a relative error of at most 0.015.
Values may be sent and summed in bfloat16 or wider, within the bound.
A program may use at most 64 MiB of HBM per device.

v0:
```python
import jax
import jax.numpy as jnp
from jax import lax
from jax.sharding import PartitionSpec as P

SUBLEN = 64
epsilon = 1e-06


def passed_along(shard, axis, by):
    size = lax.axis_size(axis)
    pairs = [(i, i + by) for i in range(size) if 0 <= i + by < size]
    return lax.ppermute(shard, axis, pairs)


def from_everyone(shard, axis):
    copies = jnp.broadcast_to(shard, (lax.axis_size(axis), *shard.shape))
    return lax.all_to_all(copies, axis, split_axis=0, concat_axis=0, tiled=True)


def of_everyone(shard, axis):
    everything = from_everyone(shard, axis)
    return jnp.sum(everything, axis=0)


def inner_step(carried, pieces):
    query_unit, key_unit, values, log_decay, strengths = pieces
    sub_len = query_unit.shape[0]
    head_dim = query_unit.shape[1]
    cumulative = jnp.cumsum(log_decay)
    positions = jnp.arange(sub_len)
    lower_mask = positions[:, None] >= positions[None, :]
    strict_mask = positions[:, None] > positions[None, :]
    spread = jnp.where(lower_mask, cumulative[:, None] - cumulative[None, :], 0.0)
    decays = jnp.where(lower_mask, jnp.exp(spread), 0.0)
    key_gram = jnp.dot(key_unit, key_unit.T)
    system = jnp.eye(sub_len, dtype=jnp.float32) + jnp.where(
        strict_mask, strengths[:, None] * decays * key_gram, 0.0
    )
    right_side = jnp.concatenate(
        [(strengths * jnp.exp(cumulative))[:, None] * key_unit, strengths[:, None] * values], axis=1
    )
    solved = jax.scipy.linalg.solve_triangular(system, right_side, lower=True, unit_diagonal=True)
    new_values = solved[:, head_dim:] - jnp.dot(solved[:, :head_dim], carried)
    scores = decays * jnp.dot(query_unit, key_unit.T)
    output = jnp.dot(query_unit * jnp.exp(cumulative)[:, None], carried) + jnp.dot(
        scores, new_values
    )
    tail_decay = jnp.exp(cumulative[-1] - cumulative)
    updated = jnp.exp(cumulative[-1]) * carried + jnp.dot(
        (key_unit * tail_decay[:, None]).T, new_values
    )
    return (updated, output)


def core(query_row, key_row, values, gate_a, gate_b, params, initial):
    length = query_row.shape[0]
    head_dim = query_row.shape[1]
    query_unit = (
        query_row
        * lax.rsqrt(jnp.sum(query_row * query_row, axis=-1, keepdims=True) + epsilon)
        * head_dim ** (-0.5)
    )
    key_unit = key_row * lax.rsqrt(jnp.sum(key_row * key_row, axis=-1, keepdims=True) + epsilon)
    log_decay = -jnp.exp(params[0]) * jax.nn.softplus(gate_a + params[1])
    strengths = jax.nn.sigmoid(gate_b)
    blocks = length // SUBLEN

    def into_blocks(array):
        return array.reshape((blocks, SUBLEN) + array.shape[1:])

    final_state, outputs = lax.scan(
        inner_step,
        initial,
        (
            into_blocks(query_unit),
            into_blocks(key_unit),
            into_blocks(values),
            into_blocks(log_decay),
            into_blocks(strengths),
        ),
    )
    return (outputs.reshape(length, head_dim), final_state)


def core_heads(query_rows, key_rows, values, gate_a, gate_b, params, initial):
    mapped = jax.vmap(core, in_axes=(0, 0, 0, 0, 0, 1, 0))
    return mapped(query_rows, key_rows, values, gate_a, gate_b, params, initial)


def per_device(
    layer_input, value_weight, query_raw, key_raw, out_grad, gate_logits, decay_params, saved_states
):
    tokens_all = lax.all_gather(layer_input, "tp", axis=1, tiled=True)[0]
    length = tokens_all.shape[0]
    head_dim = saved_states.shape[-1]
    head_count = query_raw.shape[2] // head_dim
    weight_full = lax.all_gather(value_weight, ("dp", "ctx"), axis=0, tiled=True)
    value_flat = jnp.dot(tokens_all, weight_full, preferred_element_type=jnp.float32)
    value_round = value_flat.astype(jnp.bfloat16)

    def split_heads(flat_rows):
        return (
            flat_rows.reshape(length, head_count, head_dim).transpose(1, 0, 2).astype(jnp.float32)
        )

    query_heads = split_heads(query_raw[0])
    key_heads = split_heads(key_raw[0])
    value_heads = split_heads(value_round)
    decay_logit = gate_logits[0, 0]
    strength_logit = gate_logits[1, 0]
    initial_states = saved_states[0, 0]
    outputs, pullback = jax.vjp(
        core_heads,
        query_heads,
        key_heads,
        value_heads,
        decay_logit,
        strength_logit,
        decay_params,
        initial_states,
    )
    cotangent = split_heads(out_grad[0])
    zeros_state = jnp.zeros_like(initial_states)
    incoming = zeros_state
    for section_index in range(lax.axis_size("ctx") - 1):
        leaving = pullback((cotangent, incoming))[6]
        incoming = passed_along(leaving.astype(jnp.bfloat16), "ctx", -1).astype(leaving.dtype)
    gradients = pullback((cotangent, incoming))
    query_grad = (
        gradients[0]
        .transpose(1, 0, 2)
        .reshape(length, head_count * head_dim)
        .astype(jnp.bfloat16)[None]
    )
    key_grad = (
        gradients[1]
        .transpose(1, 0, 2)
        .reshape(length, head_count * head_dim)
        .astype(jnp.bfloat16)[None]
    )
    value_grad = (
        gradients[2].transpose(1, 0, 2).reshape(length, head_count * head_dim).astype(jnp.bfloat16)
    )
    gate_grad = jnp.stack([gradients[3], gradients[4]])[:, None]
    decay_grad = of_everyone(gradients[5], ("dp", "ctx"))
    summed = lax.psum_scatter(
        lax.dot_general(
            value_grad, weight_full, (((1,), (1,)), ((), ())), preferred_element_type=jnp.float32
        ).astype(jnp.bfloat16),
        "tp",
        scatter_dimension=0,
        tiled=True,
    )
    input_grad = summed[None]
    return (input_grad, query_grad, key_grad, gate_grad, decay_grad)


def solution(mesh):
    placed = (
        P("dp", ("ctx", "tp"), None),
        P(("dp", "ctx"), "tp"),
        P("dp", "ctx", "tp"),
        P("dp", "ctx", "tp"),
        P("dp", "ctx", "tp"),
        P(None, "dp", "tp", "ctx"),
        P(None, "tp"),
        P("dp", "ctx", "tp", None, None),
    )
    return jax.shard_map(
        per_device,
        mesh=mesh,
        in_specs=placed,
        out_specs=(
            P("dp", ("ctx", "tp"), None),
            P("dp", "ctx", "tp"),
            P("dp", "ctx", "tp"),
            P(None, "dp", "tp", "ctx"),
            P(None, "tp"),
        ),
        check_vma=False,
    )
```

profile of v0, /device:TPU:4, one launch (start us, length us, event | category | flops | bytes accessed | tf_op | source)
XLA Modules:
  0.0 489.7 jit_solution(7759611729738571562)
XLA Ops:
  9.8 1.0 copy.211
  11.1 1.0 copy.215
  13.5 79.9 %all-gather.3.cloned.1.call-done = bf16[1,256,8192]{2,1,0:T(8,128)(2,1)} async-done(((bf16[1,16,8192]{2,1,0:T(8,128)(2,1)}), bf16[1,256,8192]{2,1,0:T(8,128)(2,1)}) %all-gather.3.cloned.1.call-update) | async-done | bytes 4194320 | tf_op jit(solution)/shard_map/all_gather | solution.py:94
  93.4 74.9 %all-gather.5.cloned.1.call-done = bf16[8192,256]{1,0:T(8,128)(2,1)} async-done(((bf16[256,256]{1,0:T(8,128)(2,1)}), bf16[8192,256]{1,0:T(8,128)(2,1)}) %all-gather.5.cloned.1.call-update) | async-done | bytes 4194320 | tf_op jit(solution)/shard_map/all_gather | solution.py:98
  168.3 5.2 %fusion.210 = bf16[256,256]{0,1:T(8,128)(2,1)S(1)} fusion(bf16[8192,256]{1,0:T(8,128)(2,1)} %all-gather.5.cloned.1.call-done, bf16[1,256,8192]{2,1,0:T(8,128)(2,1)} %all-gather.3.cloned.1.call-done), kind=kOutput, calls=%fused_computation.286 | convolution fusion | flops 1073807360 | bytes 8519680 | tf_op jit(solution)/shard_map/dot_general | solution.py:99
  174.3 1.0 copy.218
  175.3 68.9 %while.135 = (s32[]{:T(128)}, f32[2,128,128]{2,1,0:T(8,128)S(1)}, f32[4,2,64,64]{3,2,1,0:T(8,128)}, bf16[4,2,128,64]{2,3,1,0:T(8,128)(2,1)S(1)}, f32[4,2,64,64]{...) while((s32[]{:T(128)}, f32[2,128,128]{2,1,0:T(8,128)S(1)}, ...), condition=%wide.region_4.5_spmd.clone.clone, body=%wide.region_2.4_spmd.clone.clone.sunk | while | flops 38195776 | bytes 3009961 | solution.py:72
  176.9 9.8 %custom-call.50 = f32[2,1,64,64]{2,3,1,0:T(8,128)S(1)} custom-call(f32[2,1,64,64]{3,2,1,0:T(8,128)S(1)} %add_bitcast_fusion.4), custom_call_target="InvertDiagBlocksLowerTriangular" | custom-call | tf_op jit(solution)/shard_map/jvp(vmap())/while/body/eval_jaxpr/jit(_solve_triangular)/triangular_solve | solution.py:43
  186.8 1.0 bitcast_dynamic-update-slice_fusion.20
  191.4 1.1 dynamic_update_slice.338
  194.1 9.8 %custom-call.50 = f32[2,1,64,64]{2,3,1,0:T(8,128)S(1)} custom-call(f32[2,1,64,64]{3,2,1,0:T(8,128)S(1)} %add_bitcast_fusion.4), custom_call_target="InvertDiagBlocksLowerTriangular" | custom-call | tf_op jit(solution)/shard_map/jvp(vmap())/while/body/eval_jaxpr/jit(_solve_triangular)/triangular_solve | solution.py:43
  208.6 1.1 dynamic_update_slice.338
  211.3 9.8 %custom-call.50 = f32[2,1,64,64]{2,3,1,0:T(8,128)S(1)} custom-call(f32[2,1,64,64]{3,2,1,0:T(8,128)S(1)} %add_bitcast_fusion.4), custom_call_target="InvertDiagBlocksLowerTriangular" | custom-call | tf_op jit(solution)/shard_map/jvp(vmap())/while/body/eval_jaxpr/jit(_solve_triangular)/triangular_solve | solution.py:43
  221.3 1.0 bitcast_dynamic-update-slice_fusion.20
  225.8 1.1 dynamic_update_slice.338
  228.6 9.8 %custom-call.50 = f32[2,1,64,64]{2,3,1,0:T(8,128)S(1)} custom-call(f32[2,1,64,64]{3,2,1,0:T(8,128)S(1)} %add_bitcast_fusion.4), custom_call_target="InvertDiagBlocksLowerTriangular" | custom-call | tf_op jit(solution)/shard_map/jvp(vmap())/while/body/eval_jaxpr/jit(_solve_triangular)/triangular_solve | solution.py:43
  243.1 1.1 dynamic_update_slice.338
  244.2 5.2 %while.137 = (s32[]{:T(128)}, f32[2,128,128]{2,1,0:T(8,128)S(1)}, f32[4,2,1,1]{1,3,2,0:T(1,128)}, bf16[4,2,64,128]{3,2,1,0:T(8,128)(2,1)S(1)}, bf16[4,2,64,128]{...) while((s32[]{:T(128)}, f32[2,128,128]{2,1,0:T(8,128)S(1)}, ...), condition=%wide.region_6.7_spmd.clone, body=%wide.region_5.6_spmd.clone.sunk | while | flops 14893060 | bytes 986779 | solution.py:72
  249.4 1.3 collective-permute-start
  250.7 1.8 collective-permute-done
  252.6 5.2 %while.133 = (s32[]{:T(128)}, f32[2,128,128]{2,1,0:T(8,128)S(1)}, f32[4,2,1,1]{1,3,2,0:T(1,128)}, bf16[4,2,64,128]{3,2,1,0:T(8,128)(2,1)S(1)}, bf16[4,2,64,128]{...) while((s32[]{:T(128)}, f32[2,128,128]{2,1,0:T(8,128)S(1)}, ...), condition=%wide.region_8.9_spmd, body=%wide.region_7.8_spmd.sunk | while | flops 14827523 | bytes 986249 | solution.py:72
  257.8 1.3 collective-permute-start.1
  259.1 3.9 collective-permute-done.1
  263.1 5.2 %while.134 = (s32[]{:T(128)}, f32[2,128,128]{2,1,0:T(8,128)S(1)}, f32[4,2,1,1]{1,3,2,0:T(1,128)}, bf16[4,2,64,128]{3,2,1,0:T(8,128)(2,1)S(1)}, bf16[4,2,64,128]{...) while((s32[]{:T(128)}, f32[2,128,128]{2,1,0:T(8,128)S(1)}, ...), condition=%wide.region_10.11_spmd, body=%wide.region_9.10_spmd.sunk | while | flops 14827523 | bytes 986249 | solution.py:72
  268.3 1.3 collective-permute-start.2
  270.2 3.6 collective-permute-done.2
  275.9 96.7 %while.136 = (s32[]{:T(128)}, f32[2,128,128]{2,1,0:T(8,128)S(1)}, f32[4,2,64,128]{3,2,0,1:T(8,128)}, f32[4,2,64,128]{3,2,0,1:T(8,128)}, bf16[4,2,64,128]{3,2,0,1...) while((s32[]{:T(128)}, f32[2,128,128]{2,1,0:T(8,128)S(1)}, ...), condition=%wide.region_22.23_spmd.clone.clone, body=%wide.region_11.22_spmd.clone.clone.sunk | while | flops 95114432 | bytes 4842541 | solution.py:72
  276.4 1.2 fusion.376
  279.4 9.8 %custom-call.51 = f32[2,1,64,64]{2,3,1,0:T(8,128)S(1)} custom-call(f32[2,1,64,64]{3,2,1,0:T(8,128)S(1)} %add_bitcast_fusion.5), custom_call_target="InvertDiagBlocksLowerTriangular" | custom-call | tf_op jit(solution)/shard_map/transpose(jvp(vmap()))/while/body/eval_jaxpr/jit(_solve_triangular)/triangular_solve | solution.py:43
  289.9 1.2 fusion.377
  291.6 1.0 fusion.372
  300.5 1.2 fusion.376
  303.6 9.8 %custom-call.51 = f32[2,1,64,64]{2,3,1,0:T(8,128)S(1)} custom-call(f32[2,1,64,64]{3,2,1,0:T(8,128)S(1)} %add_bitcast_fusion.5), custom_call_target="InvertDiagBlocksLowerTriangular" | custom-call | tf_op jit(solution)/shard_map/transpose(jvp(vmap()))/while/body/eval_jaxpr/jit(_solve_triangular)/triangular_solve | solution.py:43
  314.1 1.2 fusion.377
  315.7 1.0 fusion.372
  324.7 1.2 fusion.376
  327.8 9.8 %custom-call.51 = f32[2,1,64,64]{2,3,1,0:T(8,128)S(1)} custom-call(f32[2,1,64,64]{3,2,1,0:T(8,128)S(1)} %add_bitcast_fusion.5), custom_call_target="InvertDiagBlocksLowerTriangular" | custom-call | tf_op jit(solution)/shard_map/transpose(jvp(vmap()))/while/body/eval_jaxpr/jit(_solve_triangular)/triangular_solve | solution.py:43
  338.3 1.2 fusion.377
  339.9 1.0 fusion.372
  348.9 1.2 fusion.376
  352.0 9.8 %custom-call.51 = f32[2,1,64,64]{2,3,1,0:T(8,128)S(1)} custom-call(f32[2,1,64,64]{3,2,1,0:T(8,128)S(1)} %add_bitcast_fusion.5), custom_call_target="InvertDiagBlocksLowerTriangular" | custom-call | tf_op jit(solution)/shard_map/transpose(jvp(vmap()))/while/body/eval_jaxpr/jit(_solve_triangular)/triangular_solve | solution.py:43
  362.5 1.2 fusion.377
  364.1 1.0 fusion.372
  372.6 1.0 copy.234
  373.7 5.5 %convolution_convert_fusion = bf16[256,8192]{1,0:T(8,128)(2,1)} fusion(bf16[256,256]{0,1:T(8,128)(2,1)S(1)} %bitcast.659, bf16[8192,256]{1,0:T(8,128)(2,1)} %all-gather.5.cloned.1.call-done), kind=kOutput, calls=%fused_computation.283 | convolution fusion | flops 1075838976 | bytes 8519680 | tf_op jit(solution)/shard_map/dot_general | solution.py:148
  380.7 8.6 %all-to-all-start = ((f32[32,2,2]{2,1,0:T(2,128)}), f32[32,2,2]{2,1,0:T(2,128)S(1)}, u32[]{:S(2)}, u32[]{:S(2)}) async-start(f32[32,2,2]{2,1,0:T(2,128)} %broadcast_in_dim.279), calls=%async_computation.1 | async-start | bytes 65536 | tf_op jit(solution)/shard_map/all_to_all | solution.py:18
  392.3 5.3 %all-to-all-done = f32[32,2,2]{2,1,0:T(2,128)S(1)} async-done(((f32[32,2,2]{2,1,0:T(2,128)}), f32[32,2,2]{2,1,0:T(2,128)S(1)}, u32[]{:S(2)}, u32[]{:S(2)}) %all-to-all-start) | async-done | bytes 544 | tf_op jit(solution)/shard_map/all_to_all | solution.py:18
  398.2 85.0 %reduce-scatter.2.cloned.1.call-done = bf16[16,8192]{1,0:T(8,128)(2,1)} async-done(((bf16[256,8192]{1,0:T(8,128)(2,1)}), bf16[16,8192]{1,0:T(8,128)(2,1)}) %reduce-scatter.2.cloned.1.call-update) | async-done | bytes 262160 | tf_op jit(solution)/shard_map/reduce_scatter | solution.py:147
  (404 shorter events, 93.8 us)
Async XLA Ops:
  7.2 5.2 %copy-start.3 = (bf16[1,256,256]{2,1,0:T(8,128)(2,1)S(1)}, bf16[1,256,256]{2,1,0:T(8,128)(2,1)}, u32[]{:S(2)}) copy-start(bf16[1,256,256]{2,1,0:T(8,128)(2,1)} %param.22) | copy-start | bytes 393220
  7.2 5.6 %copy-start.19 = (f32[2,2]{1,0:T(2,128)S(1)}, f32[2,2]{1,0:T(2,128)}, u32[]{:S(2)}) copy-start(f32[2,2]{1,0:T(2,128)} %param.24) | copy-start | bytes 52
  7.2 86.2 %all-gather.3.cloned.1.call-start = ((), (), s32[]{:S(2)}) async-start(), calls=%async_computation.2 | async-start | bytes 4456448 | tf_op jit(solution)/shard_map/all_gather | solution.py:94
  7.9 160.4 %all-gather.5.cloned.1.call-start = ((), (), s32[]{:S(2)}) async-start(), calls=%async_computation.3 | async-start | bytes 4325376 | tf_op jit(solution)/shard_map/all_gather | solution.py:98
  8.7 474.5 %reduce-scatter.2.cloned.1.call-start = ((), (), s32[]{:S(2)}) async-start(), calls=%async_computation.4 | async-start | bytes 4456448 | tf_op jit(solution)/shard_map/reduce_scatter | solution.py:147
  9.6 2.5 copy-start.10
  10.9 1.8 copy-start.6
  10.9 1.7 copy-start.4
  12.1 0.6 copy-start.8
  12.8 160.7 %copy-start.15 = (f32[2]{0:T(128)}, f32[2]{0:T(128)S(1)}, u32[]{:S(2)}) copy-start(f32[2]{0:T(128)S(1)} %get-tuple-element.2979) | copy-start | bytes 28
  12.8 160.7 %copy-start.17 = (f32[2]{0:T(128)}, f32[2]{0:T(128)S(1)}, u32[]{:S(2)}) copy-start(f32[2]{0:T(128)S(1)} %get-tuple-element.2980) | copy-start | bytes 28
  13.5 161.8 %copy-start = (f32[1,1,2,128,128]{4,3,2,1,0:T(8,128)S(1)}, f32[1,1,2,128,128]{4,3,2,1,0:T(8,128)}, u32[]{:S(2)}) copy-start(f32[1,1,2,128,128]{4,3,2,1,0:T(8,128)} %param.25) | copy-start | bytes 393220
  249.4 3.1 collective-permute-start
  257.8 5.3 %collective-permute-start.1 = (bf16[2,128,128]{2,1,0:T(8,128)(2,1)S(1)}, bf16[2,128,128]{2,1,0:T(8,128)(2,1)S(1)}, u32[]{:S(2)}, u32[]{:S(2)}) collective-permute-start(bf16[2,128,128]{2,1,0:T(8,128)(2,1)S(1)} %convert_element_type.127), channel_id=1, source_target_pairs={{16,0},{32,16},{48,32},{17,1},{33,17},{49,33},{18,2},{34,18},{50,3... | collective-permute-start | bytes 196616 | tf_op jit(solution)/shard_map/ppermute | solution.py:13
  268.3 5.6 %collective-permute-start.2 = (bf16[2,128,128]{2,1,0:T(8,128)(2,1)S(1)}, bf16[2,128,128]{2,1,0:T(8,128)(2,1)S(1)}, u32[]{:S(2)}, u32[]{:S(2)}) collective-permute-start(bf16[2,128,128]{2,1,0:T(8,128)(2,1)S(1)} %convert_element_type.129), channel_id=1, source_target_pairs={{16,0},{32,16},{48,32},{17,1},{33,17},{49,33},{18,2},{34,18},{50,3... | collective-permute-start | bytes 196616 | tf_op jit(solution)/shard_map/ppermute | solution.py:13
  379.1 0.7 copy-start.12
  379.1 0.7 copy-start.16
  379.1 0.7 copy-start.18
  379.1 0.9 copy-start.20
  379.1 10.1 %copy-start.13 = (f32[4,2,64]{2,1,0:T(2,128)S(1)}, f32[4,2,64]{2,1,0:T(2,128)}, u32[]{:S(2)}) copy-start(f32[4,2,64]{2,1,0:T(2,128)} %get-tuple-element.1874) | copy-start | bytes 6148
  379.1 10.3 %copy-start.2 = (f32[4,2,64,128]{3,2,0,1:T(8,128)S(1)}, f32[4,2,64,128]{3,2,0,1:T(8,128)}, u32[]{:S(2)}) copy-start(f32[4,2,64,128]{3,2,0,1:T(8,128)} %get-tuple-element.1872) | copy-start | bytes 786436
  379.2 10.4 %copy-start.1 = (f32[4,2,64,128]{3,2,0,1:T(8,128)S(1)}, f32[4,2,64,128]{3,2,0,1:T(8,128)}, u32[]{:S(2)}) copy-start(f32[4,2,64,128]{3,2,0,1:T(8,128)} %get-tuple-element.1871) | copy-start | bytes 786436
  379.2 10.7 %copy-start.11 = (f32[1,1,2,256]{3,2,1,0:T(2,128)S(1)}, f32[1,1,2,256]{3,2,1,0:T(2,128)}, u32[]{:S(2)}) copy-start(f32[1,1,2,256]{3,2,1,0:T(2,128)} %copy-done.10) | copy-start | bytes 6148
  379.2 10.7 %copy-start.7 = (f32[2,256]{1,0:T(2,128)S(1)}, f32[2,256]{1,0:T(2,128)}, u32[]{:S(2)}) copy-start(f32[2,256]{1,0:T(2,128)} %copy-done.6) | copy-start | bytes 6148
  379.2 10.7 %copy-start.14 = (f32[2,1,2,256]{3,2,1,0:T(2,128)S(1)}, f32[2,1,2,256]{3,2,1,0:T(2,128)}, u32[]{:S(2)}) copy-start(f32[2,1,2,256]{3,2,1,0:T(2,128)} %param.23) | copy-start | bytes 12292
  379.2 10.8 %copy-start.9 = (f32[2,256]{1,0:T(2,128)S(1)}, f32[2,256]{1,0:T(2,128)}, u32[]{:S(2)}) copy-start(f32[2,256]{1,0:T(2,128)} %copy-done.8) | copy-start | bytes 6148
  379.2 10.8 %copy-start.5 = (f32[2,256]{1,0:T(2,128)S(1)}, f32[2,256]{1,0:T(2,128)}, u32[]{:S(2)}) copy-start(f32[2,256]{1,0:T(2,128)} %copy-done.4) | copy-start | bytes 6148
  380.7 16.9 %all-to-all-start = ((f32[32,2,2]{2,1,0:T(2,128)}), f32[32,2,2]{2,1,0:T(2,128)S(1)}, u32[]{:S(2)}, u32[]{:S(2)}) async-start(f32[32,2,2]{2,1,0:T(2,128)} %broadcast_in_dim.279), calls=%async_computation.1 | async-start | bytes 65536 | tf_op jit(solution)/shard_map/all_to_all | solution.py:18
Sparse Core Ops, SparseCore 0:
  11.0 82.3 all-gather.2
  95.6 72.6 all-gather.4
  379.4 103.7 reduce-scatter.1
where the time goes:
time: 492 us; the launch traced here: 490 us
  waiting for transfers between devices  256 us (52%)
  other arithmetic  102 us (21%)
  matrix products  63.2 us (13%)
  local copies, waits for them, and re-layouts  40.8 us (8%)
  between operations  14.5 us (3%)
  starting transfers between devices  12.6 us (3%)
    reduce_scatter x1, waiting for transfers between devices, per_device(): lax.psum_scatter(lax.dot_general(value_grad, weight_full, (((1,), (1,)),...  85 us
    another operation x36, other arithmetic, inner_step(): jax.scipy.linalg.solve_triangular(system, right_side, lower=True, unit_di...  83.2 us
    all_gather x1, waiting for transfers between devices, per_device(): tokens_all = lax.all_gather(layer_input, 'tp', axis=1, tiled=True)[0]  79.9 us
    all_gather x1, waiting for transfers between devices, per_device(): lax.all_gather(value_weight, ('dp', 'ctx'), axis=0, tiled=True)  74.9 us
    mul x16, local copies, waits for them, and re-layouts, inner_step(): jnp.exp(cumulative[-1]) * carried  10.1 us
    another operation x12, matrix products, inner_step(): jax.scipy.linalg.solve_triangular(system, right_side, lower=True, unit_di...  9.85 us
  transfers between devices with their start and end apart: 7, of which 7 were waited for; matrix products, arithmetic and copies ran while one was open for 2% of the time, Pallas kernels for 0%

commit v1 on v0

--- a/solution.py
+++ b/solution.py
@@ -5,6 +5,13 @@
 
 SUBLEN = 64
 epsilon = 1e-06
+
+
+def step_on_state(local_x):
+    crops = []
+    for _ in range(lax.axis_size(("dp", "ctx"))):
+        crops.append(local_x)
+    return jnp.concatenate(lax.all_to_all(jnp.stack(crops, axis=0), ("dp", "ctx"), 0, 0), 0)
 
 
 def passed_along(shard, axis, by):
@@ -95,7 +102,7 @@
     length = tokens_all.shape[0]
     head_dim = saved_states.shape[-1]
     head_count = query_raw.shape[2] // head_dim
-    weight_full = lax.all_gather(value_weight, ("dp", "ctx"), axis=0, tiled=True)
+    weight_full = step_on_state(value_weight)
     value_flat = jnp.dot(tokens_all, weight_full, preferred_element_type=jnp.float32)
     value_round = value_flat.astype(jnp.bfloat16)
 

time: 492 us -> 453 us (0.921)
  the two profiles are of different devices: /device:TPU:4 before, /device:TPU:6 now
where the time goes in v1:
time: 453 us; the launch traced here: 451 us
  waiting for transfers between devices  200 us (44%)
  other arithmetic  101 us (22%)
  matrix products  63.5 us (14%)
  local copies, waits for them, and re-layouts  43.8 us (10%)
  starting transfers between devices  26.3 us (6%)
  between operations  14.8 us (3%)
    all_gather x1, waiting for transfers between devices, per_device(): tokens_all = lax.all_gather(layer_input, 'tp', axis=1, tiled=True)[0]  102 us
    another operation x36, other arithmetic, inner_step(): jax.scipy.linalg.solve_triangular(system, right_side, lower=True, unit_di...  83.2 us
    reduce_scatter x1, waiting for transfers between devices, per_device(): lax.psum_scatter(lax.dot_general(value_grad, weight_full, (((1,), (1,)),...  83.1 us
    all_to_all x1, starting transfers between devices, step_on_state(): lax.all_to_all(jnp.stack(crops, axis=0), ('dp', 'ctx'), 0, 0)  12 us
    all_to_all x1, starting transfers between devices, from_everyone(): return lax.all_to_all(copies, axis, split_axis=0, concat_axis=0, tiled=True)  10.3 us
    another operation x12, matrix products, inner_step(): jax.scipy.linalg.solve_triangular(system, right_side, lower=True, unit_di...  9.9 us
    mul x16, local copies, waits for them, and re-layouts, inner_step(): jnp.exp(cumulative[-1]) * carried  9.88 us
    ppermute x3, waiting for transfers between devices, passed_along(): return lax.ppermute(shard, axis, pairs)  9.17 us
  transfers between devices with their start and end apart: 7, of which 6 were waited for; matrix products, arithmetic and copies ran while one was open for 2% of the time, Pallas kernels for 0%

profile of v1, /device:TPU:6, one launch (start us, length us, event | category | flops | bytes accessed | tf_op | source)
XLA Modules:
  0.0 450.7 jit_solution(3547780723759245740)
XLA Ops:
  7.2 3.3 stack.4
  10.5 12.0 %all-to-all-start = ((bf16[32,256,256]{2,1,0:T(8,128)(2,1)}), bf16[32,256,256]{2,1,0:T(8,128)(2,1)}, u32[]{:S(2)}, u32[]{:S(2)}) async-start(bf16[32,256,256]{2,1,0:T(8,128)(2,1)} %stack.4), calls=%async_computation | async-start | bytes 8388608 | tf_op jit(solution)/shard_map/all_to_all | solution.py:14
  24.5 1.0 copy.220
  26.4 101.9 %all-gather.2.cloned.1.call-done = bf16[1,256,8192]{2,1,0:T(8,128)(2,1)} async-done(((bf16[1,16,8192]{2,1,0:T(8,128)(2,1)}), bf16[1,256,8192]{2,1,0:T(8,128)(2,1)}) %all-gather.2.cloned.1.call-update) | async-done | bytes 4194320 | tf_op jit(solution)/shard_map/all_gather | solution.py:101
  128.3 5.2 %fusion.210 = bf16[256,256]{0,1:T(8,128)(2,1)S(1)} fusion(bf16[8192,256]{1,0:T(8,128)(2,1)} %bitcast.23, bf16[1,256,8192]{2,1,0:T(8,128)(2,1)} %all-gather.2.cloned.1.call-done), kind=kOutput, calls=%fused_computation.286 | convolution fusion | flops 1073807360 | bytes 8519680 | tf_op jit(solution)/shard_map/dot_general | solution.py:106
  135.4 69.5 %while.135 = (s32[]{:T(128)}, f32[2,128,128]{2,1,0:T(8,128)S(1)}, f32[4,2,64,64]{3,2,1,0:T(8,128)}, bf16[4,2,128,64]{2,3,1,0:T(8,128)(2,1)S(1)}, f32[4,2,64,64]{...) while((s32[]{:T(128)}, f32[2,128,128]{2,1,0:T(8,128)S(1)}, ...), condition=%wide.region_4.5_spmd.clone.clone, body=%wide.region_2.4_spmd.clone.clone.sunk | while | flops 38195776 | bytes 3009961 | solution.py:79
  137.0 9.8 %custom-call.50 = f32[2,1,64,64]{2,3,1,0:T(8,128)S(1)} custom-call(f32[2,1,64,64]{3,2,1,0:T(8,128)S(1)} %add_bitcast_fusion.4), custom_call_target="InvertDiagBlocksLowerTriangular" | custom-call | tf_op jit(solution)/shard_map/jvp(vmap())/while/body/eval_jaxpr/jit(_solve_triangular)/triangular_solve | solution.py:50
  146.9 1.0 bitcast_dynamic-update-slice_fusion.20
  151.5 1.3 dynamic_update_slice.338
  154.3 9.8 %custom-call.50 = f32[2,1,64,64]{2,3,1,0:T(8,128)S(1)} custom-call(f32[2,1,64,64]{3,2,1,0:T(8,128)S(1)} %add_bitcast_fusion.4), custom_call_target="InvertDiagBlocksLowerTriangular" | custom-call | tf_op jit(solution)/shard_map/jvp(vmap())/while/body/eval_jaxpr/jit(_solve_triangular)/triangular_solve | solution.py:50
  168.8 1.3 dynamic_update_slice.338
  171.7 9.8 %custom-call.50 = f32[2,1,64,64]{2,3,1,0:T(8,128)S(1)} custom-call(f32[2,1,64,64]{3,2,1,0:T(8,128)S(1)} %add_bitcast_fusion.4), custom_call_target="InvertDiagBlocksLowerTriangular" | custom-call | tf_op jit(solution)/shard_map/jvp(vmap())/while/body/eval_jaxpr/jit(_solve_triangular)/triangular_solve | solution.py:50
  181.6 1.0 bitcast_dynamic-update-slice_fusion.20
  186.2 1.3 dynamic_update_slice.338
  189.1 9.8 %custom-call.50 = f32[2,1,64,64]{2,3,1,0:T(8,128)S(1)} custom-call(f32[2,1,64,64]{3,2,1,0:T(8,128)S(1)} %add_bitcast_fusion.4), custom_call_target="InvertDiagBlocksLowerTriangular" | custom-call | tf_op jit(solution)/shard_map/jvp(vmap())/while/body/eval_jaxpr/jit(_solve_triangular)/triangular_solve | solution.py:50
  199.0 1.0 bitcast_dynamic-update-slice_fusion.20
  203.6 1.3 dynamic_update_slice.338
  204.9 5.1 %while.137 = (s32[]{:T(128)}, f32[2,128,128]{2,1,0:T(8,128)S(1)}, f32[4,2,1,1]{1,3,2,0:T(1,128)}, bf16[4,2,64,128]{3,2,1,0:T(8,128)(2,1)S(1)}, bf16[4,2,64,128]{...) while((s32[]{:T(128)}, f32[2,128,128]{2,1,0:T(8,128)S(1)}, ...), condition=%wide.region_6.7_spmd.clone, body=%wide.region_5.6_spmd.clone.sunk | while | flops 14893060 | bytes 986779 | solution.py:79
  210.1 1.3 collective-permute-start
  211.4 1.8 collective-permute-done
  213.2 5.1 %while.133 = (s32[]{:T(128)}, f32[2,128,128]{2,1,0:T(8,128)S(1)}, f32[4,2,1,1]{1,3,2,0:T(1,128)}, bf16[4,2,64,128]{3,2,1,0:T(8,128)(2,1)S(1)}, bf16[4,2,64,128]{...) while((s32[]{:T(128)}, f32[2,128,128]{2,1,0:T(8,128)S(1)}, ...), condition=%wide.region_8.9_spmd, body=%wide.region_7.8_spmd.sunk | while | flops 14827523 | bytes 986249 | solution.py:79
  218.4 1.3 collective-permute-start.1
  219.7 3.7 collective-permute-done.1
  223.5 5.1 %while.134 = (s32[]{:T(128)}, f32[2,128,128]{2,1,0:T(8,128)S(1)}, f32[4,2,1,1]{1,3,2,0:T(1,128)}, bf16[4,2,64,128]{3,2,1,0:T(8,128)(2,1)S(1)}, bf16[4,2,64,128]{...) while((s32[]{:T(128)}, f32[2,128,128]{2,1,0:T(8,128)S(1)}, ...), condition=%wide.region_10.11_spmd, body=%wide.region_9.10_spmd.sunk | while | flops 14827523 | bytes 986249 | solution.py:79
  228.6 1.3 collective-permute-start.2
  230.6 3.6 collective-permute-done.2
  236.3 97.1 %while.136 = (s32[]{:T(128)}, f32[2,128,128]{2,1,0:T(8,128)S(1)}, f32[4,2,64,128]{3,2,0,1:T(8,128)}, f32[4,2,64,128]{3,2,0,1:T(8,128)}, bf16[4,2,64,128]{3,2,0,1...) while((s32[]{:T(128)}, f32[2,128,128]{2,1,0:T(8,128)S(1)}, ...), condition=%wide.region_22.23_spmd.clone.clone, body=%wide.region_11.22_spmd.clone.clone.sunk | while | flops 95114432 | bytes 4842541 | solution.py:79
  236.7 1.2 fusion.376
  239.7 9.8 %custom-call.51 = f32[2,1,64,64]{2,3,1,0:T(8,128)S(1)} custom-call(f32[2,1,64,64]{3,2,1,0:T(8,128)S(1)} %add_bitcast_fusion.5), custom_call_target="InvertDiagBlocksLowerTriangular" | custom-call | tf_op jit(solution)/shard_map/transpose(jvp(vmap()))/while/body/eval_jaxpr/jit(_solve_triangular)/triangular_solve | solution.py:50
  250.3 1.2 fusion.377
  251.9 1.0 fusion.372
  261.0 1.2 fusion.376
  264.0 9.8 %custom-call.51 = f32[2,1,64,64]{2,3,1,0:T(8,128)S(1)} custom-call(f32[2,1,64,64]{3,2,1,0:T(8,128)S(1)} %add_bitcast_fusion.5), custom_call_target="InvertDiagBlocksLowerTriangular" | custom-call | tf_op jit(solution)/shard_map/transpose(jvp(vmap()))/while/body/eval_jaxpr/jit(_solve_triangular)/triangular_solve | solution.py:50
  274.5 1.2 fusion.377
  276.1 1.0 fusion.372
  285.3 1.2 fusion.376
  288.3 9.8 %custom-call.51 = f32[2,1,64,64]{2,3,1,0:T(8,128)S(1)} custom-call(f32[2,1,64,64]{3,2,1,0:T(8,128)S(1)} %add_bitcast_fusion.5), custom_call_target="InvertDiagBlocksLowerTriangular" | custom-call | tf_op jit(solution)/shard_map/transpose(jvp(vmap()))/while/body/eval_jaxpr/jit(_solve_triangular)/triangular_solve | solution.py:50
  298.9 1.2 fusion.377
  300.5 1.0 fusion.372
  309.5 1.2 fusion.376
  312.6 9.8 %custom-call.51 = f32[2,1,64,64]{2,3,1,0:T(8,128)S(1)} custom-call(f32[2,1,64,64]{3,2,1,0:T(8,128)S(1)} %add_bitcast_fusion.5), custom_call_target="InvertDiagBlocksLowerTriangular" | custom-call | tf_op jit(solution)/shard_map/transpose(jvp(vmap()))/while/body/eval_jaxpr/jit(_solve_triangular)/triangular_solve | solution.py:50
  323.1 1.2 fusion.377
  324.7 1.0 fusion.372
  333.4 1.0 copy.234
  334.4 5.5 %convolution_convert_fusion = bf16[256,8192]{1,0:T(8,128)(2,1)} fusion(bf16[256,256]{0,1:T(8,128)(2,1)S(1)} %bitcast.660, bf16[8192,256]{1,0:T(8,128)(2,1)} %bitcast.23), kind=kOutput, calls=%fused_computation.283 | convolution fusion | flops 1075838976 | bytes 8519680 | tf_op jit(solution)/shard_map/dot_general | solution.py:155
  341.4 10.3 %all-to-all-start.1 = ((f32[32,2,2]{2,1,0:T(2,128)}), f32[32,2,2]{2,1,0:T(2,128)S(1)}, u32[]{:S(2)}, u32[]{:S(2)}) async-start(f32[32,2,2]{2,1,0:T(2,128)} %broadcast_in_dim.279), calls=%async_computation.2 | async-start | bytes 65536 | tf_op jit(solution)/shard_map/all_to_all | solution.py:25
  354.8 5.3 %all-to-all-done.1 = f32[32,2,2]{2,1,0:T(2,128)S(1)} async-done(((f32[32,2,2]{2,1,0:T(2,128)}), f32[32,2,2]{2,1,0:T(2,128)S(1)}, u32[]{:S(2)}, u32[]{:S(2)}) %all-to-all-start.1) | async-done | bytes 544 | tf_op jit(solution)/shard_map/all_to_all | solution.py:25
  360.7 83.1 %reduce-scatter.2.cloned.1.call-done = bf16[16,8192]{1,0:T(8,128)(2,1)} async-done(((bf16[256,8192]{1,0:T(8,128)(2,1)}), bf16[16,8192]{1,0:T(8,128)(2,1)}) %reduce-scatter.2.cloned.1.call-update) | async-done | bytes 262160 | tf_op jit(solution)/shard_map/reduce_scatter | solution.py:154
  (408 shorter events, 92.7 us)
Async XLA Ops:
  10.5 13.0 %copy-start.15 = (f32[2,1,2,256]{3,2,1,0:T(2,128)S(1)}, f32[2,1,2,256]{3,2,1,0:T(2,128)}, u32[]{:S(2)}) copy-start(f32[2,1,2,256]{3,2,1,0:T(2,128)} %param.23) | copy-start | bytes 12292
  10.5 13.2 %copy-start.3 = (bf16[1,256,256]{2,1,0:T(8,128)(2,1)S(1)}, bf16[1,256,256]{2,1,0:T(8,128)(2,1)}, u32[]{:S(2)}) copy-start(bf16[1,256,256]{2,1,0:T(8,128)(2,1)} %param.21) | copy-start | bytes 393220
  10.5 13.6 %copy-start.4 = (bf16[1,256,256]{2,1,0:T(8,128)(2,1)S(1)}, bf16[1,256,256]{2,1,0:T(8,128)(2,1)}, u32[]{:S(2)}) copy-start(bf16[1,256,256]{2,1,0:T(8,128)(2,1)} %param.20) | copy-start | bytes 393220
  10.5 117.8 %all-to-all-start = ((bf16[32,256,256]{2,1,0:T(8,128)(2,1)}), bf16[32,256,256]{2,1,0:T(8,128)(2,1)}, u32[]{:S(2)}, u32[]{:S(2)}) async-start(bf16[32,256,256]{2,1,0:T(8,128)(2,1)} %stack.4), calls=%async_computation | async-start | bytes 8388608 | tf_op jit(solution)/shard_map/all_to_all | solution.py:14
  22.5 3.2 copy-start.21
  22.5 105.8 %all-gather.2.cloned.1.call-start = ((), (), s32[]{:S(2)}) async-start(), calls=%async_computation.3 | async-start | bytes 4456448 | tf_op jit(solution)/shard_map/all_gather | solution.py:101
  23.2 420.6 %reduce-scatter.2.cloned.1.call-start = ((), (), s32[]{:S(2)}) async-start(), calls=%async_computation.4 | async-start | bytes 4456448 | tf_op jit(solution)/shard_map/reduce_scatter | solution.py:154
  23.5 0.7 copy-start.11
  23.9 1.8 copy-start.7
  23.9 1.7 copy-start.5
  24.2 1.4 copy-start.9
  25.7 107.9 %copy-start.17 = (f32[2]{0:T(128)}, f32[2]{0:T(128)S(1)}, u32[]{:S(2)}) copy-start(f32[2]{0:T(128)S(1)} %get-tuple-element.2979) | copy-start | bytes 28
  25.7 107.9 %copy-start.19 = (f32[2]{0:T(128)}, f32[2]{0:T(128)S(1)}, u32[]{:S(2)}) copy-start(f32[2]{0:T(128)S(1)} %get-tuple-element.2980) | copy-start | bytes 28
  128.3 7.0 %copy-start = (f32[1,1,2,128,128]{4,3,2,1,0:T(8,128)S(1)}, f32[1,1,2,128,128]{4,3,2,1,0:T(8,128)}, u32[]{:S(2)}) copy-start(f32[1,1,2,128,128]{4,3,2,1,0:T(8,128)} %param.25) | copy-start | bytes 393220
  210.1 3.1 collective-permute-start
  218.4 5.1 %collective-permute-start.1 = (bf16[2,128,128]{2,1,0:T(8,128)(2,1)S(1)}, bf16[2,128,128]{2,1,0:T(8,128)(2,1)S(1)}, u32[]{:S(2)}, u32[]{:S(2)}) collective-permute-start(bf16[2,128,128]{2,1,0:T(8,128)(2,1)S(1)} %convert_element_type.127), channel_id=1, source_target_pairs={{16,0},{32,16},{48,32},{17,1},{33,17},{49,33},{18,2},{34,18},{50,3... | collective-permute-start | bytes 196616 | tf_op jit(solution)/shard_map/ppermute | solution.py:20
  228.6 5.6 %collective-permute-start.2 = (bf16[2,128,128]{2,1,0:T(8,128)(2,1)S(1)}, bf16[2,128,128]{2,1,0:T(8,128)(2,1)S(1)}, u32[]{:S(2)}, u32[]{:S(2)}) collective-permute-start(bf16[2,128,128]{2,1,0:T(8,128)(2,1)S(1)} %convert_element_type.129), channel_id=1, source_target_pairs={{16,0},{32,16},{48,32},{17,1},{33,17},{49,33},{18,2},{34,18},{50,3... | collective-permute-start | bytes 196616 | tf_op jit(solution)/shard_map/ppermute | solution.py:20
  339.9 0.7 copy-start.13
  339.9 0.7 copy-start.18
  339.9 0.7 copy-start.20
  339.9 0.9 copy-start.22
  339.9 11.9 %copy-start.14 = (f32[4,2,64]{2,1,0:T(2,128)S(1)}, f32[4,2,64]{2,1,0:T(2,128)}, u32[]{:S(2)}) copy-start(f32[4,2,64]{2,1,0:T(2,128)} %get-tuple-element.1874) | copy-start | bytes 6148
  339.9 12.1 %copy-start.2 = (f32[4,2,64,128]{3,2,0,1:T(8,128)S(1)}, f32[4,2,64,128]{3,2,0,1:T(8,128)}, u32[]{:S(2)}) copy-start(f32[4,2,64,128]{3,2,0,1:T(8,128)} %get-tuple-element.1872) | copy-start | bytes 786436
  339.9 12.2 %copy-start.1 = (f32[4,2,64,128]{3,2,0,1:T(8,128)S(1)}, f32[4,2,64,128]{3,2,0,1:T(8,128)}, u32[]{:S(2)}) copy-start(f32[4,2,64,128]{3,2,0,1:T(8,128)} %get-tuple-element.1871) | copy-start | bytes 786436
  339.9 12.4 %copy-start.12 = (f32[1,1,2,256]{3,2,1,0:T(2,128)S(1)}, f32[1,1,2,256]{3,2,1,0:T(2,128)}, u32[]{:S(2)}) copy-start(f32[1,1,2,256]{3,2,1,0:T(2,128)} %copy-done.11) | copy-start | bytes 6148
  339.9 12.5 %copy-start.8 = (f32[2,256]{1,0:T(2,128)S(1)}, f32[2,256]{1,0:T(2,128)}, u32[]{:S(2)}) copy-start(f32[2,256]{1,0:T(2,128)} %copy-done.7) | copy-start | bytes 6148
  339.9 12.5 %copy-start.16 = (f32[2,1,2,256]{3,2,1,0:T(2,128)S(1)}, f32[2,1,2,256]{3,2,1,0:T(2,128)}, u32[]{:S(2)}) copy-start(f32[2,1,2,256]{3,2,1,0:T(2,128)} %param.23) | copy-start | bytes 12292
  339.9 12.6 %copy-start.10 = (f32[2,256]{1,0:T(2,128)S(1)}, f32[2,256]{1,0:T(2,128)}, u32[]{:S(2)}) copy-start(f32[2,256]{1,0:T(2,128)} %copy-done.9) | copy-start | bytes 6148
  340.0 12.6 %copy-start.6 = (f32[2,256]{1,0:T(2,128)S(1)}, f32[2,256]{1,0:T(2,128)}, u32[]{:S(2)}) copy-start(f32[2,256]{1,0:T(2,128)} %copy-done.5) | copy-start | bytes 6148
  341.4 18.6 %all-to-all-start.1 = ((f32[32,2,2]{2,1,0:T(2,128)}), f32[32,2,2]{2,1,0:T(2,128)S(1)}, u32[]{:S(2)}, u32[]{:S(2)}) async-start(f32[32,2,2]{2,1,0:T(2,128)} %broadcast_in_dim.279), calls=%async_computation.2 | async-start | bytes 65536 | tf_op jit(solution)/shard_map/all_to_all | solution.py:25
Sparse Core Ops, SparseCore 0:
  26.3 101.9 all-gather.1
  340.1 103.6 reduce-scatter.1
